TPU v7x, 32 devices: a whole 2x2x4 slice. The times are simulated.
32 devices in a mesh: row: 4 (over y, x), col: 8 (over z, core).
Axes of the slice: x: 2, y: 2, z: 4, core: 2. Of those that a mesh axis runs over, the one named last changes fastest.
Arguments:
- model_gradient: float32 [3, 512, 512, 256], P(None, 'row', 'col'), may hold values from -6 to 6
- filter_x: float32 [512, 512], replicated, may hold values from 0 to 1, as said below
- filter_y: float32 [512, 512], replicated, may hold values from 0 to 1, as said below
- filter_z: float32 [256, 256], replicated, may hold values from 0 to 1, as said below
- depth_scale: float32 [3, 256], replicated, may hold values from 0.3 to 3
Outputs:
- smoothed: float32 [3, 512, 512, 256], P(None, 'row', 'col')
Inputs may be any that keep to these rules, and one draw needn't show every extreme that they name: `filter_x`: each row is a nonnegative smoothing kernel of its own width plus one half on the diagonal; rows sum to one. `filter_y`: each row is a nonnegative smoothing kernel of its own width plus one half on the diagonal; rows sum to one. `filter_z`: each row is a nonnegative smoothing kernel of its own width plus one half on the diagonal; rows sum to one.
All inputs are finite; a program needn't handle non-finite values.
Results may differ from a plain program's by a relative error of at most 0.0001.
Values sent between devices are 32-bit elements; how exact they have to be, the bound alone decides.
A program may use at most 192 MiB of HBM per device.

v0:
```python
import jax
import jax.numpy as jnp
from jax import lax
from jax.experimental import pallas as pl
from jax.experimental.pallas import tpu as pltpu
from jax.sharding import PartitionSpec as P

ACCURACY = lax.Precision.HIGH
AXES = ("row", "col")
LAST = (((1,), (1,)), ((), ()))
INNER = (((1,), (0,)), ((), ()))


def split_outside(value):
    high = lax.reduce_precision(value, 8, 7)
    return high.astype(jnp.bfloat16), (value - high).astype(jnp.bfloat16)


def split(value):
    high = value.astype(jnp.bfloat16)
    return high, (value - high.astype(jnp.float32)).astype(jnp.bfloat16)


def dot3(left, right, dims):
    def one(a, b):
        return lax.dot_general(a, b, dims, preferred_element_type=jnp.float32)

    return one(left[0], right[0]) + (one(left[0], right[1]) + one(left[1], right[0]))


def cost(flops, count):
    return pl.CostEstimate(flops=flops, bytes_accessed=count, transcendentals=0)


def depth_kernel(high_ref, low_ref, field_ref, out_ref):
    _, xloc, tile, depth = field_ref.shape
    parts, _, block, _ = out_ref.shape
    filters = (high_ref[0], low_ref[0])
    for b in range(tile):
        piece = split(field_ref[0, :, b, :])
        column = dot3(filters, piece, LAST)
        out_ref[:, b] = column.reshape(parts, block, xloc)


def depth_pass(index, high, low, field, parts, tile):
    _, xloc, yloc, depth = field.shape
    block = depth // parts
    return pl.pallas_call(
        depth_kernel,
        grid=(yloc // tile,),
        in_specs=[
            pl.BlockSpec((1, depth, depth), lambda j: (index, 0, 0)),
            pl.BlockSpec((1, depth, depth), lambda j: (index, 0, 0)),
            pl.BlockSpec((1, xloc, tile, depth), lambda j: (index, 0, j, 0)),
        ],
        out_specs=pl.BlockSpec((parts, tile, block, xloc), lambda j: (0, j, 0, 0)),
        out_shape=jax.ShapeDtypeStruct((parts, yloc, block, xloc), jnp.float32),
        cost_estimate=cost(6 * xloc * yloc * depth * depth, 8 * xloc * yloc * depth),
    )(high, low, field)


def first_kernel(high_ref, low_ref, in_ref, out_ref):
    rows, _, yloc, block, xloc = in_ref.shape
    flat = [in_ref[r, 0].reshape(yloc * block, xloc) for r in range(rows)]
    piece = split(jnp.concatenate(flat, axis=1))
    for r in range(rows):
        part = pl.ds(r * xloc, xloc)
        value = dot3(piece, (high_ref[part, :], low_ref[part, :]), LAST)
        out_ref[r, 0] = value.reshape(yloc, block, xloc)


def first_pass(high, low, field):
    rows, cols, yloc, block, xloc = field.shape
    size = rows * xloc
    spec = pl.BlockSpec((rows, 1, yloc, block, xloc), lambda s: (0, s, 0, 0, 0))
    whole = pl.BlockSpec((size, size), lambda s: (0, 0))
    return pl.pallas_call(
        first_kernel,
        grid=(cols,),
        in_specs=[whole, whole, spec],
        out_specs=spec,
        out_shape=jax.ShapeDtypeStruct(field.shape, jnp.float32),
        cost_estimate=cost(6 * size * field.size, 8 * field.size),
    )(high, low, field)


def second_kernel(high_ref, low_ref, in_ref, out_ref):
    _, cols, yloc, block, xloc = in_ref.shape
    size = cols * yloc
    filters = (high_ref[...], low_ref[...])
    for k in range(0, block, 2):
        pair = [in_ref[0, :, :, k + n, :].reshape(size, xloc) for n in range(2)]
        value = dot3(filters, split(jnp.concatenate(pair, axis=1)), INNER)
        for n in range(2):
            part = value[:, n * xloc : (n + 1) * xloc]
            out_ref[0, :, :, k + n, :] = part.reshape(cols, yloc, xloc)


def second_pass(high, low, field):
    rows, cols, yloc, block, xloc = field.shape
    size = cols * yloc
    spec = pl.BlockSpec((1, cols, yloc, block, xloc), lambda r: (r, 0, 0, 0, 0))
    whole = pl.BlockSpec((size, size), lambda r: (0, 0))
    return pl.pallas_call(
        second_kernel,
        grid=(rows,),
        in_specs=[whole, whole, spec],
        out_specs=spec,
        out_shape=jax.ShapeDtypeStruct(field.shape, jnp.float32),
        cost_estimate=cost(6 * size * field.size, 8 * field.size),
    )(high, low, field)


def place_kernel(in_ref, *refs):
    out_ref = refs[-1]
    parts, tile, block, xloc = in_ref.shape
    for j in range(tile):
        plane = in_ref[:, j].reshape(parts * block, xloc)
        out_ref[0, :, j, :] = plane.T


def place(index, params, field, output, tile):
    parts, yloc, block, xloc = field.shape
    depth = parts * block
    given = [] if output is None else [output]
    return pl.pallas_call(
        place_kernel,
        grid=(yloc // tile,),
        in_specs=[pl.BlockSpec((parts, tile, block, xloc), lambda j: (0, j, 0, 0))]
        + [pl.BlockSpec(memory_space=pl.ANY) for _ in given],
        out_specs=pl.BlockSpec((1, xloc, tile, depth), lambda j: (index, 0, j, 0)),
        out_shape=jax.ShapeDtypeStruct((params, xloc, yloc, depth), jnp.float32),
        input_output_aliases={1: 0} if given else {},
        cost_estimate=cost(0, 8 * field.size),
    )(field, *given)


def kernel_shards(model_gradient, filter_x, filter_y, filter_z, depth_scale):
    rows, cols = lax.axis_size("row"), lax.axis_size("col")
    params, xloc, yloc, depth = model_gradient.shape
    parts = rows * cols
    block = depth // parts
    scaled = split_outside(depth_scale[:, :, None] * filter_z[None, :, :])
    pair_x, pair_y = split_outside(filter_x), split_outside(filter_y)
    arrived = []
    for index in range(params):
        outgoing = depth_pass(index, *scaled, model_gradient, parts, 8)
        arrived.append(
            lax.all_to_all(outgoing, AXES, split_axis=0, concat_axis=0, tiled=True)
        )
    output = None
    for index in range(params):
        field = arrived[index].reshape(rows, cols, yloc, block, xloc)
        field = second_pass(*pair_y, first_pass(*pair_x, field))
        field = field.reshape(parts, yloc, block, xloc)
        back = lax.all_to_all(field, AXES, split_axis=0, concat_axis=0, tiled=True)
        output = place(index, params, back, output, 8)
    return output


def plane_filter(incoming, filter_x, filter_y, rows, cols):
    xloc, yloc = incoming.shape[0], incoming.shape[1]
    matrix_x = filter_x.reshape(rows, xloc, rows, xloc)
    matrix_y = filter_y.reshape(cols, yloc, cols, yloc)
    partial_value = jnp.einsum(
        "ABRa,abRSz->ABbSz", matrix_x, incoming, precision=ACCURACY
    )
    return jnp.einsum(
        "CDSb,ABbSz->ACBDz", matrix_y, partial_value, precision=ACCURACY
    )


def plain_shards(model_gradient, filter_x, filter_y, filter_z, depth_scale):
    rows, cols = lax.axis_size("row"), lax.axis_size("col")
    params, xloc, yloc, depth = model_gradient.shape
    parts = rows * cols
    block = depth // parts
    arrived = []
    for index in range(params):
        scaled_filter = depth_scale[index][:, None] * filter_z
        column = jnp.einsum(
            "kz,abz->abk", scaled_filter, model_gradient[index], precision=ACCURACY
        )
        outgoing = column.reshape(xloc, yloc, parts, block)
        arrived.append(
            lax.all_to_all(outgoing, AXES, split_axis=2, concat_axis=2, tiled=True)
        )
    results = []
    for index in range(params):
        incoming = arrived[index].reshape(xloc, yloc, rows, cols, block)
        planes = plane_filter(incoming, filter_x, filter_y, rows, cols)
        planes = planes.reshape(parts, xloc, yloc, block)
        back = lax.all_to_all(planes, AXES, split_axis=0, concat_axis=3, tiled=True)
        results.append(back.reshape(xloc, yloc, depth))
    return jnp.stack(results)


def shards(model_gradient, filter_x, filter_y, filter_z, depth_scale):
    _, xloc, yloc, depth = model_gradient.shape
    block = depth // (lax.axis_size("row") * lax.axis_size("col"))
    aligned = block % 8 == 0 and xloc % 128 == 0 and yloc % 8 == 0
    chosen = kernel_shards if aligned else plain_shards
    return chosen(model_gradient, filter_x, filter_y, filter_z, depth_scale)


def solution(mesh):
    return jax.shard_map(
        shards,
        mesh=mesh,
        in_specs=(P(None, "row", "col", None), P(), P(), P(), P()),
        out_specs=P(None, "row", "col", None),
        check_vma=False,
    )
```

profile of v0, /device:TPU:0, one launch (start us, length us, event | category | flops | bytes accessed | tf_op | source)
XLA Modules:
  0.0 1179.0 jit_solution(420466932309976594)
XLA Ops:
  2.1 32.0 %shard_map.61 = f32[32,64,8,128]{3,2,1,0:T(8,128)} custom-call(bf16[3,256,256]{2,1,0:T(8,128)(2,1)} %get-tuple-element.10.high_ref, bf16[3,256,256]{2,1,0:T(8,128)(2,1)} %get-tuple-element.9.low_ref, f32[3,128,64,256]{3,2,1,0:T(8,128)} %field_ref.5), custom_call_target="tpu_custom_call" | custom-call | flops 3221225472 | bytes 16777216 | tf_op jit(solution)/shard_map/pallas_call | solution.py:48
  34.1 7.5 all-to-all-start.4
  41.5 32.1 %shard_map.58 = f32[32,64,8,128]{3,2,1,0:T(8,128)} custom-call(bf16[3,256,256]{2,1,0:T(8,128)(2,1)} %get-tuple-element.10.high_ref, bf16[3,256,256]{2,1,0:T(8,128)(2,1)} %get-tuple-element.9.low_ref, f32[3,128,64,256]{3,2,1,0:T(8,128)} %field_ref.5), custom_call_target="tpu_custom_call" | custom-call | flops 3221225472 | bytes 16777216 | tf_op jit(solution)/shard_map/pallas_call | solution.py:48
  73.6 152.7 %all-to-all-done.4 = f32[32,64,8,128]{3,2,1,0:T(8,128)} async-done(((f32[32,64,8,128]{3,2,1,0:T(8,128)}), f32[32,64,8,128]{3,2,1,0:T(8,128)}, u32[]{:S(2)}, u32[]{:S(2)}) %all-to-all-start.4) | async-done | bytes 8388640 | tf_op jit(solution)/shard_map/all_to_all | solution.py:149
  226.3 3.7 all-to-all-start.2
  230.0 32.0 %shard_map.55 = f32[32,64,8,128]{3,2,1,0:T(8,128)} custom-call(bf16[3,256,256]{2,1,0:T(8,128)(2,1)} %get-tuple-element.10.high_ref, bf16[3,256,256]{2,1,0:T(8,128)(2,1)} %get-tuple-element.9.low_ref, f32[3,128,64,256]{3,2,1,0:T(8,128)} %field_ref.5), custom_call_target="tpu_custom_call" | custom-call | flops 3221225472 | bytes 16777216 | tf_op jit(solution)/shard_map/pallas_call | solution.py:48
  262.0 152.8 %all-to-all-done.2 = f32[32,64,8,128]{3,2,1,0:T(8,128)} async-done(((f32[32,64,8,128]{3,2,1,0:T(8,128)}), f32[32,64,8,128]{3,2,1,0:T(8,128)}, u32[]{:S(2)}, u32[]{:S(2)}) %all-to-all-start.2) | async-done | bytes 8388640 | tf_op jit(solution)/shard_map/all_to_all | solution.py:149
  414.8 3.9 all-to-all-start
  421.0 17.0 %shard_map.62.in_ref = f32[4,8,64,8,128]{4,3,2,1,0:T(8,128)} custom-call(bf16[512,512]{1,0:T(8,128)(2,1)} %get-tuple-element.6.high_ref, bf16[512,512]{1,0:T(8,128)(2,1)} %get-tuple-element.5.low_ref, f32[4,8,64,8,128]{4,3,2,1,0:T(8,128)} %bitcast.4.in_ref), custom_call_target="tpu_custom_call" | custom-call | flops 6442450944 | bytes 16777216 | tf_op jit(solution)/shard_map/pallas_call | solution.py:77
  438.0 17.4 %shard_map.63 = f32[4,8,64,8,128]{4,3,2,1,0:T(8,128)} custom-call(bf16[512,512]{1,0:T(8,128)(2,1)} %get-tuple-element.8.high_ref, bf16[512,512]{1,0:T(8,128)(2,1)} %get-tuple-element.7.low_ref, f32[4,8,64,8,128]{4,3,2,1,0:T(8,128)} %shard_map.62.in_ref), custom_call_target="tpu_custom_call" | custom-call | flops 6442450944 | bytes 16777216 | tf_op jit(solution)/shard_map/pallas_call | solution.py:104
  455.5 147.8 %all-to-all-done = f32[32,64,8,128]{3,2,1,0:T(8,128)} async-done(((f32[32,64,8,128]{3,2,1,0:T(8,128)}), f32[32,64,8,128]{3,2,1,0:T(8,128)}, u32[]{:S(2)}, u32[]{:S(2)}) %all-to-all-start) | async-done | bytes 8388640 | tf_op jit(solution)/shard_map/all_to_all | solution.py:149
  603.3 3.7 all-to-all-start.5
  607.0 17.1 %shard_map.59.in_ref = f32[4,8,64,8,128]{4,3,2,1,0:T(8,128)} custom-call(bf16[512,512]{1,0:T(8,128)(2,1)} %get-tuple-element.6.high_ref, bf16[512,512]{1,0:T(8,128)(2,1)} %get-tuple-element.5.low_ref, f32[4,8,64,8,128]{4,3,2,1,0:T(8,128)} %bitcast.2.in_ref), custom_call_target="tpu_custom_call" | custom-call | flops 6442450944 | bytes 16777216 | tf_op jit(solution)/shard_map/pallas_call | solution.py:77
  624.0 17.4 %shard_map.60 = f32[4,8,64,8,128]{4,3,2,1,0:T(8,128)} custom-call(bf16[512,512]{1,0:T(8,128)(2,1)} %get-tuple-element.8.high_ref, bf16[512,512]{1,0:T(8,128)(2,1)} %get-tuple-element.7.low_ref, f32[4,8,64,8,128]{4,3,2,1,0:T(8,128)} %shard_map.59.in_ref), custom_call_target="tpu_custom_call" | custom-call | flops 6442450944 | bytes 16777216 | tf_op jit(solution)/shard_map/pallas_call | solution.py:104
  641.4 150.4 %all-to-all-done.5.in_ref = f32[32,64,8,128]{3,2,1,0:T(8,128)} async-done(((f32[32,64,8,128]{3,2,1,0:T(8,128)}), f32[32,64,8,128]{3,2,1,0:T(8,128)}, u32[]{:S(2)}, u32[]{:S(2)}) %all-to-all-start.5) | async-done | bytes 8388640 | tf_op jit(solution)/shard_map/all_to_all | solution.py:156
  791.8 3.9 all-to-all-start.3
  795.7 17.1 %shard_map.56.in_ref = f32[4,8,64,8,128]{4,3,2,1,0:T(8,128)} custom-call(bf16[512,512]{1,0:T(8,128)(2,1)} %get-tuple-element.6.high_ref, bf16[512,512]{1,0:T(8,128)(2,1)} %get-tuple-element.5.low_ref, f32[4,8,64,8,128]{4,3,2,1,0:T(8,128)} %bitcast.in_ref), custom_call_target="tpu_custom_call" | custom-call | flops 6442450944 | bytes 16777216 | tf_op jit(solution)/shard_map/pallas_call | solution.py:77
  812.7 17.4 %shard_map.57 = f32[4,8,64,8,128]{4,3,2,1,0:T(8,128)} custom-call(bf16[512,512]{1,0:T(8,128)(2,1)} %get-tuple-element.8.high_ref, bf16[512,512]{1,0:T(8,128)(2,1)} %get-tuple-element.7.low_ref, f32[4,8,64,8,128]{4,3,2,1,0:T(8,128)} %shard_map.56.in_ref), custom_call_target="tpu_custom_call" | custom-call | flops 6442450944 | bytes 16777216 | tf_op jit(solution)/shard_map/pallas_call | solution.py:104
  830.2 150.1 %all-to-all-done.3.in_ref = f32[32,64,8,128]{3,2,1,0:T(8,128)} async-done(((f32[32,64,8,128]{3,2,1,0:T(8,128)}), f32[32,64,8,128]{3,2,1,0:T(8,128)}, u32[]{:S(2)}, u32[]{:S(2)}) %all-to-all-start.3) | async-done | bytes 8388640 | tf_op jit(solution)/shard_map/all_to_all | solution.py:156
  980.2 3.7 all-to-all-start.1
  983.9 10.3 shard_map.64.refs_0_
  994.2 10.3 shard_map.65.refs_0_
  1004.5 164.2 %all-to-all-done.1.in_ref = f32[32,64,8,128]{3,2,1,0:T(8,128)} async-done(((f32[32,64,8,128]{3,2,1,0:T(8,128)}), f32[32,64,8,128]{3,2,1,0:T(8,128)}, u32[]{:S(2)}, u32[]{:S(2)}) %all-to-all-start.1) | async-done | bytes 8388640 | tf_op jit(solution)/shard_map/all_to_all | solution.py:156
  1168.7 10.3 shard_map.66
  (7 shorter events, 4.4 us)
Async XLA Ops:
  34.1 192.2 %all-to-all-start.4 = ((f32[32,64,8,128]{3,2,1,0:T(8,128)}), f32[32,64,8,128]{3,2,1,0:T(8,128)}, u32[]{:S(2)}, u32[]{:S(2)}) async-start(f32[32,64,8,128]{3,2,1,0:T(8,128)} %shard_map.61), calls=%async_computation.4 | async-start | bytes 16777216 | tf_op jit(solution)/shard_map/all_to_all | solution.py:149
  226.3 188.5 %all-to-all-start.2 = ((f32[32,64,8,128]{3,2,1,0:T(8,128)}), f32[32,64,8,128]{3,2,1,0:T(8,128)}, u32[]{:S(2)}, u32[]{:S(2)}) async-start(f32[32,64,8,128]{3,2,1,0:T(8,128)} %shard_map.58), calls=%async_computation.2 | async-start | bytes 16777216 | tf_op jit(solution)/shard_map/all_to_all | solution.py:149
  262.0 156.6 %copy-start = (f32[512,512]{1,0:T(8,128)S(1)}, f32[512,512]{1,0:T(8,128)}, u32[]{:S(2)}) copy-start(f32[512,512]{1,0:T(8,128)} %param.6) | copy-start | bytes 3145732
  262.0 157.8 %copy-start.1 = (f32[512,512]{1,0:T(8,128)S(1)}, f32[512,512]{1,0:T(8,128)}, u32[]{:S(2)}) copy-start(f32[512,512]{1,0:T(8,128)} %param.7) | copy-start | bytes 3145732
  414.8 188.5 %all-to-all-start = ((f32[32,64,8,128]{3,2,1,0:T(8,128)}), f32[32,64,8,128]{3,2,1,0:T(8,128)}, u32[]{:S(2)}, u32[]{:S(2)}) async-start(f32[32,64,8,128]{3,2,1,0:T(8,128)} %shard_map.55), calls=%async_computation | async-start | bytes 16777216 | tf_op jit(solution)/shard_map/all_to_all | solution.py:149
  603.3 188.5 %all-to-all-start.5 = ((f32[32,64,8,128]{3,2,1,0:T(8,128)}), f32[32,64,8,128]{3,2,1,0:T(8,128)}, u32[]{:S(2)}, u32[]{:S(2)}) async-start(f32[32,64,8,128]{3,2,1,0:T(8,128)} %bitcast.8), calls=%async_computation.5 | async-start | bytes 16777216 | tf_op jit(solution)/shard_map/all_to_all | solution.py:156
  791.8 188.5 %all-to-all-start.3 = ((f32[32,64,8,128]{3,2,1,0:T(8,128)}), f32[32,64,8,128]{3,2,1,0:T(8,128)}, u32[]{:S(2)}, u32[]{:S(2)}) async-start(f32[32,64,8,128]{3,2,1,0:T(8,128)} %bitcast.6), calls=%async_computation.3 | async-start | bytes 16777216 | tf_op jit(solution)/shard_map/all_to_all | solution.py:156
  980.2 188.5 %all-to-all-start.1 = ((f32[32,64,8,128]{3,2,1,0:T(8,128)}), f32[32,64,8,128]{3,2,1,0:T(8,128)}, u32[]{:S(2)}, u32[]{:S(2)}) async-start(f32[32,64,8,128]{3,2,1,0:T(8,128)} %bitcast.7), calls=%async_computation.1 | async-start | bytes 16777216 | tf_op jit(solution)/shard_map/all_to_all | solution.py:156
where the time goes:
time: 1180 us
  waiting for transfers between devices  918 us (78%)
  Pallas kernels  230 us (19%)
  starting transfers between devices  26.3 us (2%)
    all_to_all x3, waiting for transfers between devices, kernel_shards(): back = lax.all_to_all(field, AXES, split_axis=0, concat_axis=0, tiled=True)  465 us
    all_to_all x3, waiting for transfers between devices, kernel_shards(): lax.all_to_all(outgoing, AXES, split_axis=0, concat_axis=0, tiled=True)  453 us
    pallas_call x3, Pallas kernels, depth_pass(): pl.pallas_call(depth_kernel, grid=(yloc // tile,), in_specs=[pl.BlockSpec...  96.1 us
    pallas_call x3, Pallas kernels, second_pass(): pl.pallas_call(second_kernel, grid=(rows,), in_specs=[whole, whole, spec]...  52.2 us
    pallas_call x3, Pallas kernels, first_pass(): pl.pallas_call(first_kernel, grid=(cols,), in_specs=[whole, whole, spec],...  51.1 us
    pallas_call x3, Pallas kernels, place(): pl.pallas_call(place_kernel, grid=(yloc // tile,), in_specs=[pl.BlockSpec...  30.9 us
  transfers between devices with their start and end apart: 6, of which 6 were waited for; matrix products, arithmetic and copies ran while one was open for 0% of the time, Pallas kernels for 16%

commit v1 on v0

v1 whole, which is shorter than its diff:
```python
import functools

import jax
import jax.numpy as jnp
from jax import lax
from jax.experimental import pallas as pl
from jax.experimental.pallas import tpu as pltpu
from jax.sharding import PartitionSpec as P

ACCURACY = lax.Precision.HIGH
AXES = ("row", "col")
INNER = (((1,), (0,)), ((), ()))
MESH = pl.DeviceIdType.MESH
LANES, SUBLANES = 128, 8
STAGING_LIMIT = 48 * 2**20
VMEM_LIMIT = 62 * 2**20


def split(value):
    high = value.astype(jnp.bfloat16)
    return high, (value - high.astype(jnp.float32)).astype(jnp.bfloat16)


def dot3(left, right):
    def one(a, b):
        return lax.dot_general(a, b, INNER, preferred_element_type=jnp.float32)

    return one(left[0], right[0]) + (one(left[0], right[1]) + one(left[1], right[0]))


def wait_bytes(ref, sem):
    pltpu.make_async_copy(ref, ref, sem).wait()


def smooth_kernel(
    rows, cols, field, filter_x, filter_y, filter_z, scale, out, home,
    ybuf, xbuf, raw_x, raw_y, raw_z, raw_s, pair_x, pair_y, pair_z,
    load_sem, yf_recv, yb_recv, xf_recv, xb_recv, yf_send, yb_send, xf_send, xb_send,
):
    row, col = lax.axis_index("row"), lax.axis_index("col")
    params, xloc, yloc, depth = field.shape
    ychunks, ca = ybuf.shape[1], ybuf.shape[3]
    xchunks, cb = xbuf.shape[1], xbuf.shape[4]
    xa, yb = xloc // cols, yloc // rows

    loads = [
        pltpu.make_async_copy(given, raw, load_sem.at[n])
        for n, (given, raw) in enumerate(
            [(filter_x, raw_x), (filter_y, raw_y), (filter_z, raw_z), (scale, raw_s)]
        )
    ]
    for load in loads:
        load.start()

    barrier = pltpu.get_barrier_semaphore()

    @pl.loop(1, cols)
    def _(j):
        peer = (row, lax.rem(col + j, cols))
        pl.semaphore_signal(barrier, inc=1, device_id=peer, device_id_type=MESH)

    @pl.loop(1, rows)
    def _(j):
        peer = (lax.rem(row + j, rows), col)
        pl.semaphore_signal(barrier, inc=1, device_id=peer, device_id_type=MESH)

    pl.semaphore_wait(barrier, rows + cols - 2)

    def a_range(part, c):
        return pl.ds(part * xa + c * ca, ca)

    def b_range(part, c):
        return pl.ds(pl.multiple_of(part * yb + c * cb, SUBLANES), cb)

    def send_y(p, source):
        @pl.loop(0, ychunks)
        def _(c):
            pltpu.make_async_copy(
                source.at[p, a_range(col, c)], ybuf.at[p, c, col], yf_recv.at[p, c]
            ).start()

            @pl.loop(1, cols)
            def _(j):
                to = lax.rem(col + j, cols)
                pltpu.make_async_remote_copy(
                    source.at[p, a_range(to, c)],
                    ybuf.at[p, c, col],
                    yf_send.at[p],
                    yf_recv.at[p, c],
                    device_id=(row, to),
                    device_id_type=MESH,
                ).start()

    def return_y(p, c, target):
        pltpu.make_async_copy(
            ybuf.at[p, c, col], target.at[p, a_range(col, c)], yb_recv.at[p]
        ).start()

        @pl.loop(1, cols)
        def _(j):
            to = lax.rem(col + j, cols)
            pltpu.make_async_remote_copy(
                ybuf.at[p, c, to],
                target.at[p, a_range(col, c)],
                yb_send.at[p],
                yb_recv.at[p],
                device_id=(row, to),
                device_id_type=MESH,
            ).start()

    def send_x(p, source):
        @pl.loop(0, xchunks)
        def _(c):
            pltpu.make_async_copy(
                source.at[p, :, b_range(row, c)], xbuf.at[p, c, row], xf_recv.at[p, c]
            ).start()

            @pl.loop(1, rows)
            def _(j):
                to = lax.rem(row + j, rows)
                pltpu.make_async_remote_copy(
                    source.at[p, :, b_range(to, c)],
                    xbuf.at[p, c, row],
                    xf_send.at[p],
                    xf_recv.at[p, c],
                    device_id=(to, col),
                    device_id_type=MESH,
                ).start()

    def return_x(p, c, target):
        pltpu.make_async_copy(
            xbuf.at[p, c, row], target.at[p, :, b_range(row, c)], xb_recv.at[p]
        ).start()

        @pl.loop(1, rows)
        def _(j):
            to = lax.rem(row + j, rows)
            pltpu.make_async_remote_copy(
                xbuf.at[p, c, to],
                target.at[p, :, b_range(row, c)],
                xb_send.at[p],
                xb_recv.at[p],
                device_id=(to, col),
                device_id_type=MESH,
            ).start()

    def prepare():
        for load in loads:
            load.wait()
        for raw, pair in ((raw_x, pair_x), (raw_y, pair_y)):
            pair[0], pair[1] = split(raw[...])
        turned = raw_z[...].T
        for p in range(params):
            pair_z[p, 0], pair_z[p, 1] = split(turned * raw_s[pl.ds(p, 1), :])

    def filter_y_depth(p, c):
        wait_bytes(ybuf.at[p, c], yf_recv.at[p, c])

        @pl.loop(0, ca)
        def _(a):
            plane = ybuf[p, c, :, a].reshape(cols * yloc, depth)
            column = dot3(split(plane), (pair_z[p, 0], pair_z[p, 1]))
            value = dot3((pair_y[0], pair_y[1]), split(column))
            ybuf[p, c, :, a] = value.reshape(cols, yloc, depth)

    def filter_x_rows(p, c):
        wait_bytes(xbuf.at[p, c], xf_recv.at[p, c])
        for b in range(cb):
            plane = xbuf[p, c, :, :, b, :].reshape(rows * xloc, depth)
            value = dot3((pair_x[0], pair_x[1]), split(plane))
            xbuf[p, c, :, :, b, :] = value.reshape(rows, xloc, depth)

    @pl.loop(0, params)
    def _(q):
        x_param = lax.rem(q + 1, params)

        @pl.when(q == 0)
        def _():
            send_y(0, field)
            send_x(1, field)
            prepare()

        @pl.when(q > 0)
        def _():
            wait_bytes(home.at[q], xb_recv.at[q])
            send_y(q, home)

            @pl.when(q < params - 1)
            def _():
                send_x(q + 1, field)

            @pl.when(q == params - 1)
            def _():
                wait_bytes(home.at[0], yb_recv.at[0])
                send_x(0, home)

        @pl.loop(0, max(xchunks, ychunks))
        def _(c):
            @pl.when(c < xchunks)
            def _():
                filter_x_rows(x_param, c)

                @pl.when(x_param > 0)
                def _():
                    return_x(x_param, c, home)

                @pl.when(x_param == 0)
                def _():
                    return_x(0, c, out)

            @pl.when(c < ychunks)
            def _():
                filter_y_depth(q, c)

                @pl.when(q == 0)
                def _():
                    return_y(0, c, home)

                @pl.when(q > 0)
                def _():
                    return_y(q, c, out)

    wait_bytes(out.at[0], xb_recv.at[0])

    @pl.loop(0, params)
    def _(p):
        @pl.when(p > 0)
        def _():
            wait_bytes(out.at[p], yb_recv.at[p])

        for sem in (yf_send, yb_send):
            wait_bytes(home.at[p, pl.ds(0, xloc - xa)], sem.at[p])
        for sem in (xf_send, xb_send):
            wait_bytes(home.at[p, :, pl.ds(0, yloc - yb)], sem.at[p])


def kernel_shards(model_gradient, filter_x, filter_y, filter_z, depth_scale):
    rows, cols = lax.axis_size("row"), lax.axis_size("col")
    params, xloc, yloc, depth = model_gradient.shape
    nx, ny = filter_x.shape[0], filter_y.shape[0]
    ychunks = y_chunks(xloc // cols)
    ca = xloc // cols // ychunks
    cb = SUBLANES
    xchunks = yloc // rows // cb
    whole = pl.BlockSpec(memory_space=pl.ANY)
    full = jax.ShapeDtypeStruct(model_gradient.shape, jnp.float32)
    dma = pltpu.SemaphoreType.DMA
    flops = 6 * model_gradient.size * (nx + ny + depth)
    out, _ = pl.pallas_call(
        functools.partial(smooth_kernel, rows, cols),
        in_specs=[whole] * 5,
        out_specs=[whole, whole],
        out_shape=[full, full],
        scratch_shapes=[
            pltpu.VMEM((params, ychunks, cols, ca, yloc, depth), jnp.float32),
            pltpu.VMEM((params, xchunks, rows, xloc, cb, depth), jnp.float32),
            pltpu.VMEM(filter_x.shape, jnp.float32),
            pltpu.VMEM(filter_y.shape, jnp.float32),
            pltpu.VMEM(filter_z.shape, jnp.float32),
            pltpu.VMEM(depth_scale.shape, jnp.float32),
            pltpu.VMEM((2,) + filter_x.shape, jnp.bfloat16),
            pltpu.VMEM((2,) + filter_y.shape, jnp.bfloat16),
            pltpu.VMEM((params, 2) + filter_z.shape, jnp.bfloat16),
            dma((4,)),
            dma((params, ychunks)),
            dma((params,)),
            dma((params, xchunks)),
            dma((params,)),
            dma((params,)),
            dma((params,)),
            dma((params,)),
            dma((params,)),
        ],
        cost_estimate=pl.CostEstimate(
            flops=flops, bytes_accessed=32 * model_gradient.size, transcendentals=0
        ),
        compiler_params=pltpu.CompilerParams(
            collective_id=0, has_side_effects=True, vmem_limit_bytes=VMEM_LIMIT
        ),
    )(model_gradient, filter_x, filter_y, filter_z, depth_scale)
    return out


def y_chunks(planes):
    return 4 if planes % 4 == 0 else 1


def fits(shape, rows, cols):
    params, xloc, yloc, depth = shape
    aligned = xloc % cols == 0 and yloc % (rows * SUBLANES) == 0 and depth % LANES == 0
    staged = 2 * 4 * params * xloc * yloc * depth
    return aligned and params > 1 and staged <= STAGING_LIMIT


def plane_filter(incoming, filter_x, filter_y, rows, cols):
    xloc, yloc = incoming.shape[0], incoming.shape[1]
    matrix_x = filter_x.reshape(rows, xloc, rows, xloc)
    matrix_y = filter_y.reshape(cols, yloc, cols, yloc)
    partial_value = jnp.einsum(
        "ABRa,abRSz->ABbSz", matrix_x, incoming, precision=ACCURACY
    )
    return jnp.einsum(
        "CDSb,ABbSz->ACBDz", matrix_y, partial_value, precision=ACCURACY
    )


def plain_shards(model_gradient, filter_x, filter_y, filter_z, depth_scale):
    rows, cols = lax.axis_size("row"), lax.axis_size("col")
    params, xloc, yloc, depth = model_gradient.shape
    parts = rows * cols
    block = depth // parts
    arrived = []
    for index in range(params):
        scaled_filter = depth_scale[index][:, None] * filter_z
        column = jnp.einsum(
            "kz,abz->abk", scaled_filter, model_gradient[index], precision=ACCURACY
        )
        outgoing = column.reshape(xloc, yloc, parts, block)
        arrived.append(
            lax.all_to_all(outgoing, AXES, split_axis=2, concat_axis=2, tiled=True)
        )
    results = []
    for index in range(params):
        incoming = arrived[index].reshape(xloc, yloc, rows, cols, block)
        planes = plane_filter(incoming, filter_x, filter_y, rows, cols)
        planes = planes.reshape(parts, xloc, yloc, block)
        back = lax.all_to_all(planes, AXES, split_axis=0, concat_axis=3, tiled=True)
        results.append(back.reshape(xloc, yloc, depth))
    return jnp.stack(results)


def shards(model_gradient, filter_x, filter_y, filter_z, depth_scale):
    rows, cols = lax.axis_size("row"), lax.axis_size("col")
    chosen = kernel_shards if fits(model_gradient.shape, rows, cols) else plain_shards
    return chosen(model_gradient, filter_x, filter_y, filter_z, depth_scale)


def solution(mesh):
    return jax.shard_map(
        shards,
        mesh=mesh,
        in_specs=(P(None, "row", "col", None), P(), P(), P(), P()),
        out_specs=P(None, "row", "col", None),
        check_vma=False,
    )
```

time: 1180 us -> 1100 us (0.932)
  waiting for transfers between devices: 918 us -> 0 us
  Pallas kernels: 230 us -> 1070 us
  starting transfers between devices: 26.3 us -> 0 us
  local copies, waits for them, and re-layouts: 0.01 us -> 17.5 us
    all_to_all x6 -> x0, waiting for transfers between devices: 918 us -> none  [the longest x3 465 us: kernel_shards(): back = lax.all_to_all(field, AXES, split_axis=0, concat_axis=0, tiled=True)]
    pallas_call x12 -> x1, Pallas kernels: 230 us -> 1070 us  [kernel_shards(): pl.pallas_call(functools.partial(smooth_kernel, rows, cols), in_specs=[wh...]
    all_to_all x6 -> x0, starting transfers between devices: 26.3 us -> none  [the longest x3 15 us: kernel_shards(): lax.all_to_all(outgoing, AXES, split_axis=0, concat_axis=0, tiled=True)]
    unnamed x4 -> x1, local copies, waits for them, and re-layouts: 0.01 us -> 17.5 us
  transfers between devices with their start and end apart: 6 -> 0, of which waited for: 6 -> 0; matrix products, arithmetic and copies ran while one was open for 0% -> 0% of each run, Pallas kernels for 16% -> 0%
where the time goes in v1:
time: 1100 us; the launch traced here: 1090 us
  Pallas kernels  1070 us (97%)
  local copies, waits for them, and re-layouts  17.5 us (2%)
    pallas_call x1, Pallas kernels, kernel_shards(): pl.pallas_call(functools.partial(smooth_kernel, rows, cols), in_specs=[wh...  1070 us

profile of v1, /device:TPU:0, one launch (start us, length us, event | category | flops | bytes accessed | tf_op | source)
XLA Modules:
  0.0 1088.7 jit_solution(14680550626017255144)
XLA Ops:
  0.0 1071.2 %shard_map.55 = (f32[3,128,64,256]{3,2,1,0:T(8,128)}, f32[3,128,64,256]{3,2,1,0:T(8,128)}) custom-call(f32[3,128,64,256]{3,2,1,0:T(8,128)} %field.1, f32[512,512]{1,0:T(8,128)} %filter_x.1, f32[512,512]{1,0:T(8,128)} %filter_y.1, f32[256,256]{1,0:T(8,128)} %filter_z.1, f32[3,256]{1,0:T(4,128)} %scale.1), custom_call_target="tpu_custom_call" | custom-call | flops 48318382080 | bytes 201326592 | tf_op jit(solution)/shard_map/pallas_call | solution.py:249
  1071.2 17.5 %copy.7 = f32[3,128,64,256]{3,2,1,0:T(8,128)} copy(f32[3,128,64,256]{3,2,1,0:T(8,128)} %get-tuple-element.6) | data formatting | bytes 50331648

commit v2 on v1

--- a/solution.py
+++ b/solution.py
@@ -12,6 +12,8 @@
 INNER = (((1,), (0,)), ((), ()))
 MESH = pl.DeviceIdType.MESH
 LANES, SUBLANES = 128, 8
+PLACE_PLANES = 8
+SPARE = 2 * 2**20
 STAGING_LIMIT = 48 * 2**20
 VMEM_LIMIT = 62 * 2**20
 
@@ -33,15 +35,16 @@
 
 
 def smooth_kernel(
-    rows, cols, field, filter_x, filter_y, filter_z, scale, out, home,
+    rows, cols, tail, field, filter_x, filter_y, filter_z, scale, out, home, rest,
     ybuf, xbuf, raw_x, raw_y, raw_z, raw_s, pair_x, pair_y, pair_z,
-    load_sem, yf_recv, yb_recv, xf_recv, xb_recv, yf_send, yb_send, xf_send, xb_send,
+    load_sem, rest_sem, yf_recv, yb_recv, xf_recv, xb_recv, yf_send, yb_send, xf_send, xb_send,
 ):
     row, col = lax.axis_index("row"), lax.axis_index("col")
     params, xloc, yloc, depth = field.shape
     ychunks, ca = ybuf.shape[1], ybuf.shape[3]
     xchunks, cb = xbuf.shape[1], xbuf.shape[4]
     xa, yb = xloc // cols, yloc // rows
+    last, half = params - 1, cols // 2
 
     loads = [
         pltpu.make_async_copy(given, raw, load_sem.at[n])
@@ -96,16 +99,29 @@
             ybuf.at[p, c, col], target.at[p, a_range(col, c)], yb_recv.at[p]
         ).start()
 
+        kept = (p == last) & (c >= ychunks - tail)
+
         @pl.loop(1, cols)
         def _(j):
             to = lax.rem(col + j, cols)
-            pltpu.make_async_remote_copy(
-                ybuf.at[p, c, to],
-                target.at[p, a_range(col, c)],
-                yb_send.at[p],
-                yb_recv.at[p],
-                device_id=(row, to),
-                device_id_type=MESH,
+
+            @pl.when(jnp.logical_not(kept & (j == half)))
+            def _():
+                pltpu.make_async_remote_copy(
+                    ybuf.at[p, c, to],
+                    target.at[p, a_range(col, c)],
+                    yb_send.at[p],
+                    yb_recv.at[p],
+                    device_id=(row, to),
+                    device_id_type=MESH,
+                ).start()
+
+        @pl.when(kept)
+        def _():
+            pltpu.make_async_copy(
+                ybuf.at[p, c, lax.rem(col + half, cols)],
+                rest.at[pl.ds((c - (ychunks - tail)) * ca, ca)],
+                rest_sem,
             ).start()
 
     def send_x(p, source):
@@ -224,14 +240,93 @@
 
     @pl.loop(0, params)
     def _(p):
-        @pl.when(p > 0)
+        wait_bytes(home.at[p, pl.ds(0, xloc - xa)], yf_send.at[p])
+
+        @pl.when(p < last)
         def _():
-            wait_bytes(out.at[p], yb_recv.at[p])
-
-        for sem in (yf_send, yb_send):
-            wait_bytes(home.at[p, pl.ds(0, xloc - xa)], sem.at[p])
+            wait_bytes(home.at[p, pl.ds(0, xloc - xa)], yb_send.at[p])
+
+            @pl.when(p > 0)
+            def _():
+                wait_bytes(out.at[p], yb_recv.at[p])
+
+        @pl.when(p == last)
+        def _():
+            sent = xloc - tail * ca
+            wait_bytes(out.at[p, pl.ds(0, sent)], yb_recv.at[p])
+            wait_bytes(home.at[p, pl.ds(0, sent - xa)], yb_send.at[p])
+            wait_bytes(rest, rest_sem)
+
         for sem in (xf_send, xb_send):
             wait_bytes(home.at[p, :, pl.ds(0, yloc - yb)], sem.at[p])
+
+
+def place_kernel(given, out, slots, reads, writes):
+    count, planes = slots.shape[:2]
+    per = given.shape[1] // planes
+
+    def part(ref, n):
+        return ref.at[n // per, pl.ds(n % per * planes, planes)]
+
+    def read(n):
+        return pltpu.make_async_copy(part(given, n), slots.at[n], reads.at[n])
+
+    def write(n):
+        return pltpu.make_async_copy(slots.at[n], part(out, n), writes.at[n])
+
+    for n in range(count):
+        read(n).start()
+    for n in range(count):
+        read(n).wait()
+        write(n).start()
+    for n in range(count):
+        write(n).wait()
+
+
+def place(field):
+    params, xloc, yloc, depth = field.shape
+    planes = max(n for n in range(1, PLACE_PLANES + 1) if xloc % n == 0)
+    count = params * xloc // planes
+    return pl.pallas_call(
+        place_kernel,
+        in_specs=[pl.BlockSpec(memory_space=pl.ANY)],
+        out_specs=pl.BlockSpec(memory_space=pl.ANY),
+        out_shape=jax.ShapeDtypeStruct(field.shape, jnp.float32),
+        scratch_shapes=[
+            pltpu.VMEM((count, planes, yloc, depth), jnp.float32),
+            pltpu.SemaphoreType.DMA((count,)),
+            pltpu.SemaphoreType.DMA((count,)),
+        ],
+        cost_estimate=pl.CostEstimate(
+            flops=512 * field.size, bytes_accessed=8 * field.size, transcendentals=0
+        ),
+        compiler_params=pltpu.CompilerParams(vmem_limit_bytes=VMEM_LIMIT - SPARE),
+    )(field)
+
+
+def insert_kernel(cols, landed, _, out, sem):
+    params, xloc = out.shape[:2]
+    planes, xa = landed.shape[0], xloc // cols
+    source = lax.rem(lax.axis_index("col") + cols // 2, cols)
+    target = out.at[params - 1, pl.ds((source + 1) * xa - planes, planes)]
+    move = pltpu.make_async_copy(landed, target, sem)
+    move.start()
+    move.wait()
+
+
+def insert(field, landed, cols):
+    return pl.pallas_call(
+        functools.partial(insert_kernel, cols),
+        in_specs=[pl.BlockSpec(memory_space=pltpu.VMEM), pl.BlockSpec(memory_space=pl.ANY)],
+        out_specs=pl.BlockSpec(memory_space=pl.ANY),
+        out_shape=jax.ShapeDtypeStruct(field.shape, jnp.float32),
+        input_output_aliases={1: 0},
+        scratch_shapes=[pltpu.SemaphoreType.DMA],
+        cost_estimate=pl.CostEstimate(
+            flops=landed.size, bytes_accessed=8 * landed.size, transcendentals=0
+        ),
+        compiler_params=pltpu.CompilerParams(vmem_limit_bytes=SPARE),
+    )(landed, field)
 
 
 def kernel_shards(model_gradient, filter_x, filter_y, filter_z, depth_scale):
@@ -240,17 +335,19 @@
     nx, ny = filter_x.shape[0], filter_y.shape[0]
     ychunks = y_chunks(xloc // cols)
     ca = xloc // cols // ychunks
+    tail = max(1, ychunks // 2)
     cb = SUBLANES
     xchunks = yloc // rows // cb
     whole = pl.BlockSpec(memory_space=pl.ANY)
     full = jax.ShapeDtypeStruct(model_gradient.shape, jnp.float32)
     dma = pltpu.SemaphoreType.DMA
     flops = 6 * model_gradient.size * (nx + ny + depth)
-    out, _ = pl.pallas_call(
-        functools.partial(smooth_kernel, rows, cols),
+    held = jax.ShapeDtypeStruct((tail * ca, yloc, depth), jnp.float32)
+    out, _, rest = pl.pallas_call(
+        functools.partial(smooth_kernel, rows, cols, tail),
         in_specs=[whole] * 5,
-        out_specs=[whole, whole],
-        out_shape=[full, full],
+        out_specs=[whole] * 3,
+        out_shape=[full, full, held],
         scratch_shapes=[
             pltpu.VMEM((params, ychunks, cols, ca, yloc, depth), jnp.float32),
             pltpu.VMEM((params, xchunks, rows, xloc, cb, depth), jnp.float32),
@@ -262,6 +359,7 @@
             pltpu.VMEM((2,) + filter_y.shape, jnp.bfloat16),
             pltpu.VMEM((params, 2) + filter_z.shape, jnp.bfloat16),
             dma((4,)),
+            dma,
             dma((params, ychunks)),
             dma((params,)),
             dma((params, xchunks)),
@@ -278,7 +376,9 @@
             collective_id=0, has_side_effects=True, vmem_limit_bytes=VMEM_LIMIT
         ),
     )(model_gradient, filter_x, filter_y, filter_z, depth_scale)
-    return out
+    swap = [(s, (s + cols // 2) % cols) for s in range(cols)]
+    landed = lax.ppermute(rest, "col", swap)
+    return insert(place(out), landed, cols)
 
 
 def y_chunks(planes):
@@ -287,7 +387,8 @@
 
 def fits(shape, rows, cols):
     params, xloc, yloc, depth = shape
-    aligned = xloc % cols == 0 and yloc % (rows * SUBLANES) == 0 and depth % LANES == 0
+    aligned = cols % 2 == 0 and xloc % cols == 0 and depth % LANES == 0
+    aligned = aligned and yloc % (rows * SUBLANES) == 0
     staged = 2 * 4 * params * xloc * yloc * depth
     return aligned and params > 1 and staged <= STAGING_LIMIT
 

time: 1100 us -> 1090 us (level)
  local copies, waits for them, and re-layouts: 17.5 us -> 0 us
  starting transfers between devices: 0 us -> 11.8 us
    unnamed x1 -> x0, local copies, waits for them, and re-layouts: 17.5 us -> none
    ppermute x0 -> x1, starting transfers between devices: none -> 11.8 us  [kernel_shards(): landed = lax.ppermute(rest, 'col', swap)]
    pallas_call x1 -> x3, Pallas kernels: 1070 us -> 1070 us  [the longest x1 1050 us: kernel_shards(): pl.pallas_call(functools.partial(smooth_kernel, rows, cols, tail), in_spe...]
  transfers between devices with their start and end apart: 0 -> 1, of which waited for: 0 -> 1; matrix products, arithmetic and copies ran while one was open for 0% -> 0% of each run, Pallas kernels for 0% -> 2%
where the time goes in v2:
time: 1090 us
  Pallas kernels  1070 us (98%)
  starting transfers between devices  11.8 us (1%)
    pallas_call x1, Pallas kernels, kernel_shards(): pl.pallas_call(functools.partial(smooth_kernel, rows, cols, tail), in_spe...  1050 us
  transfers between devices with their start and end apart: 1, of which 1 were waited for; matrix products, arithmetic and copies ran while one was open for 0% of the time, Pallas kernels for 2%

profile of v2, /device:TPU:0, one launch (start us, length us, event | category | flops | bytes accessed | tf_op | source)
XLA Modules:
  0.0 1087.4 jit_solution(13729328167601545233)
XLA Ops:
  0.0 1052.2 %shard_map.55 = (f32[3,128,64,256]{3,2,1,0:T(8,128)}, f32[3,128,64,256]{3,2,1,0:T(8,128)}, f32[8,64,256]{2,1,0:T(8,128)}) custom-call(f32[3,128,64,256]{3,2,1,0:T(8,128)} %field.1, f32[512,512]{1,0:T(8,128)} %filter_x.1, f32[512,512]{1,0:T(8,128)} %filter_y.1, f32[256,256]{1,0:T(8,128)} %filter_z.1, f32[3,256]{1,0:T(4,128)} %scale.1), custom_call_target="tpu_custom_call" | custom-call | flops 48318382080 | bytes 201326592 | tf_op jit(solution)/shard_map/pallas_call | solution.py:346
  1052.2 11.8 %collective-permute-start = (f32[8,64,256]{2,1,0:T(8,128)}, f32[8,64,256]{2,1,0:T(8,128)S(1)}, u32[]{:S(2)}, u32[]{:S(2)}) collective-permute-start(f32[8,64,256]{2,1,0:T(8,128)} %get-tuple-element.7), channel_id=1, source_target_pairs={{0,4},{1,5},{2,6},{3,7},{4,0},{5,1},{6,2},{7,3},{8,12},{9,13},{10,... | collective-permute-start | bytes 1572872 | tf_op jit(solution)/shard_map/ppermute | solution.py:380
  1064.0 17.6 %shard_map.56._ = f32[3,128,64,256]{3,2,1,0:T(8,128)} custom-call(f32[3,128,64,256]{3,2,1,0:T(8,128)} %get-tuple-element.8.given), custom_call_target="tpu_custom_call" | custom-call | flops 3221225472 | bytes 50331648 | tf_op jit(solution)/shard_map/pallas_call | solution.py:290
  1081.6 5.0 collective-permute-done.landed
  1086.6 0.8 shard_map.57
Async XLA Ops:
  1052.2 34.4 %collective-permute-start = (f32[8,64,256]{2,1,0:T(8,128)}, f32[8,64,256]{2,1,0:T(8,128)S(1)}, u32[]{:S(2)}, u32[]{:S(2)}) collective-permute-start(f32[8,64,256]{2,1,0:T(8,128)} %get-tuple-element.7), channel_id=1, source_target_pairs={{0,4},{1,5},{2,6},{3,7},{4,0},{5,1},{6,2},{7,3},{8,12},{9,13},{10,... | collective-permute-start | bytes 1572872 | tf_op jit(solution)/shard_map/ppermute | solution.py:380

commit v3 on v2

--- a/solution.py
+++ b/solution.py
@@ -69,6 +69,9 @@
 
     pl.semaphore_wait(barrier, rows + cols - 2)
 
+    def far_first(j):
+        return half + (j // 2) * (1 - 2 * (j % 2))
+
     def a_range(part, c):
         return pl.ds(part * xa + c * ca, ca)
 
@@ -84,7 +87,7 @@
 
             @pl.loop(1, cols)
             def _(j):
-                to = lax.rem(col + j, cols)
+                to = lax.rem(col + far_first(j), cols)
                 pltpu.make_async_remote_copy(
                     source.at[p, a_range(to, c)],
                     ybuf.at[p, c, col],
@@ -103,9 +106,9 @@
 
         @pl.loop(1, cols)
         def _(j):
-            to = lax.rem(col + j, cols)
-
-            @pl.when(jnp.logical_not(kept & (j == half)))
+            to = lax.rem(col + far_first(j), cols)
+
+            @pl.when(jnp.logical_not(kept & (j == 1)))
             def _():
                 pltpu.make_async_remote_copy(
                     ybuf.at[p, c, to],

time: 1090 us -> 1090 us (level)
  no operation moved by 1% of the time
where the time goes in v3:
time: 1090 us
  Pallas kernels  1080 us (99%)
    pallas_call x1, Pallas kernels, kernel_shards(): pl.pallas_call(functools.partial(smooth_kernel, rows, cols, tail), in_spe...  1060 us
  transfers between devices with their start and end apart: 1, of which 1 were waited for; matrix products, arithmetic and copies ran while one was open for 0% of the time, Pallas kernels for 2%

profile of v3, /device:TPU:0, one launch (start us, length us, event | category | flops | bytes accessed | tf_op | source)
XLA Modules:
  0.0 1087.0 jit_solution(18356014643827316168)
XLA Ops:
  0.0 1057.4 %shard_map.55 = (f32[3,128,64,256]{3,2,1,0:T(8,128)}, f32[3,128,64,256]{3,2,1,0:T(8,128)}, f32[8,64,256]{2,1,0:T(8,128)}) custom-call(f32[3,128,64,256]{3,2,1,0:T(8,128)} %field.1, f32[512,512]{1,0:T(8,128)} %filter_x.1, f32[512,512]{1,0:T(8,128)} %filter_y.1, f32[256,256]{1,0:T(8,128)} %filter_z.1, f32[3,256]{1,0:T(4,128)} %scale.1), custom_call_target="tpu_custom_call" | custom-call | flops 48318382080 | bytes 201326592 | tf_op jit(solution)/shard_map/pallas_call | solution.py:349
  1057.4 8.0 collective-permute-start
  1065.4 17.6 %shard_map.56._ = f32[3,128,64,256]{3,2,1,0:T(8,128)} custom-call(f32[3,128,64,256]{3,2,1,0:T(8,128)} %get-tuple-element.8.given), custom_call_target="tpu_custom_call" | custom-call | flops 3221225472 | bytes 50331648 | tf_op jit(solution)/shard_map/pallas_call | solution.py:293
  1083.0 3.1 collective-permute-done.landed
  1086.2 0.8 shard_map.57
Async XLA Ops:
  1057.4 28.8 %collective-permute-start = (f32[8,64,256]{2,1,0:T(8,128)}, f32[8,64,256]{2,1,0:T(8,128)S(1)}, u32[]{:S(2)}, u32[]{:S(2)}) collective-permute-start(f32[8,64,256]{2,1,0:T(8,128)} %get-tuple-element.7), channel_id=1, source_target_pairs={{0,4},{1,5},{2,6},{3,7},{4,0},{5,1},{6,2},{7,3},{8,12},{9,13},{10,... | collective-permute-start | bytes 1572872 | tf_op jit(solution)/shard_map/ppermute | solution.py:383
